TPU v7x, 128 devices: a whole 4x4x4 slice. The times are simulated.
128 devices in a mesh: zg: 2 (over x_lo), xy: 64 (over x_hi, y, z, core).
Axes of the slice: x: 4 (x_hi: 2, x_lo: 2; x = x_hi * 2 + x_lo), y: 4, z: 4, core: 2. Of those that a mesh axis runs over, the one named last changes fastest.
Arguments:
- charges: float32 [262144], P(('zg', 'xy')), may hold values from -12 to 12
- cells: int32 [8, 262144], P(None, ('zg', 'xy')), may hold values from 0 to 786431
- splines: float32 [8, 262144], P(None, ('zg', 'xy')), may hold values from 0.05 to 1
- counts: int32 [128], P(('zg', 'xy')), may hold values from 1024 to 2048, as said below
- green: bfloat16 [512, 4, 384, 384], P(('zg', 'xy')), may hold values from -0.3125 to 0.3125
Outputs:
- potential: float32 [384, 512, 512], P(('zg', 'xy'))
Inputs may be any that keep to these rules, and one draw needn't show every extreme that they name: `counts`: some device has all 2048 slots live in every draw.
All inputs are finite; a program needn't handle non-finite values.
Results may differ from a plain program's by a relative error of at most 0.0041.
Values may be sent and summed in bfloat16 or wider, within the bound.
A program may use at most 64 MiB of HBM per device.

v0:
```python
import math

import jax
import jax.numpy as jnp
from jax import lax
from jax.sharding import PartitionSpec as P

NX = 512
NY = 512
NZ = 384
KYB = 4


def tables(length):
    index = jnp.arange(length, dtype=jnp.int32)
    product = index[:, None] * index[None, :] % length
    angle = product.astype(jnp.float32) * (2.0 * math.pi / length)
    return (jnp.cos(angle), jnp.sin(angle))


def shards(charges, cells, splines, counts, green):
    groups = lax.axis_size("zg")
    rows = lax.axis_size("xy")
    slab = NZ // (groups * rows)
    slots = charges.shape[0]
    live = (jnp.arange(slots, dtype=jnp.int32) < counts[0]).astype(jnp.float32)
    values = splines * (charges * live)[None, :]
    density = (
        jnp.zeros((slab * NX * NY,), jnp.float32).at[cells.reshape(-1)].add(values.reshape(-1))
    )
    density = density.reshape(slab, NX, NY)
    cos_y, sin_y = tables(NY)
    cos_x, sin_x = tables(NX)
    scale = 1.0 / math.sqrt(NX * NY)
    forward_y = jnp.stack([cos_y, -sin_y], axis=1)
    along = jnp.einsum("zxy,yev->zxev", density, forward_y, precision=lax.Precision.HIGHEST)
    forward_x = jnp.stack(
        [jnp.stack([cos_x, sin_x], axis=1), jnp.stack([-sin_x, cos_x], axis=1)], axis=0
    )
    spectrum = (
        jnp.einsum("cuex,zxev->zcuv", forward_x, along, precision=lax.Precision.HIGHEST) * scale
    ).astype(jnp.bfloat16)
    pencil = lax.all_to_all(spectrum, ("zg", "xy"), split_axis=2, concat_axis=0, tiled=True)
    depth, parts, waves, width = pencil.shape
    blocks = pencil.reshape(depth, parts, waves, KYB, width // KYB)
    mixed = jnp.einsum("abzw,wcabj->zcabj", green, blocks, preferred_element_type=jnp.float32)
    returned = lax.all_to_all(
        mixed.reshape(depth, parts, waves, width).astype(jnp.bfloat16),
        ("zg", "xy"),
        split_axis=0,
        concat_axis=2,
        tiled=True,
    )
    inverse_x = jnp.stack(
        [jnp.stack([cos_x, -sin_x], axis=1), jnp.stack([sin_x, cos_x], axis=1)], axis=1
    )
    upper_x = inverse_x.astype(jnp.bfloat16)
    lower_x = (inverse_x - upper_x.astype(jnp.float32)).astype(jnp.bfloat16)
    middle = jnp.einsum("xceu,zeuv->zxcv", upper_x, returned, preferred_element_type=jnp.float32)
    middle = middle + jnp.einsum(
        "xceu,zeuv->zxcv", lower_x, returned, preferred_element_type=jnp.float32
    )
    inverse_y = jnp.stack([cos_y, -sin_y], axis=0)
    potential = (
        jnp.einsum("zxcv,cvy->zxy", middle, inverse_y, precision=lax.Precision.HIGHEST) * scale
    )
    return potential


def solution(mesh):
    in_specs = (
        P(("zg", "xy")),
        P(None, ("zg", "xy")),
        P(None, ("zg", "xy")),
        P(("zg", "xy")),
        P(("zg", "xy"), None, None, None),
    )
    out_specs = P(("zg", "xy"), None, None)
    return jax.shard_map(shards, mesh=mesh, in_specs=in_specs, out_specs=out_specs, check_vma=False)
```

profile of v0, /device:TPU:1, one launch (start us, length us, event | category | flops | bytes accessed | tf_op | source)
XLA Modules:
  0.0 296.6 jit_solution(15891612420639336365)
XLA Ops:
  0.0 0.0 copy-start.9
  0.0 0.0 copy-start.7
  0.0 0.0 copy-start.8
  0.0 5.0 %fusion.51 = (f32[512,1,512]{2,0,1:T(8,128)}, f32[512,1,512]{2,0,1:T(8,128)}) fusion(), kind=kLoop, calls=%fused_computation.61 | loop fusion | flops 3670016 | bytes 2097152 | tf_op jit(solution)/shard_map/sin | solution.py:18
  5.0 4.6 %fusion.53 = f32[512,1,512]{2,0,1:T(8,128)} fusion(), kind=kLoop, calls=%fused_computation.63 | loop fusion | flops 3932160 | bytes 1048576 | tf_op jit(solution)/shard_map/neg | solution.py:35
  10.2 0.0 copy-done.9
  10.3 0.0 copy-done.7
  10.3 0.0 copy-done.8
  10.3 0.1 copy.48
  10.4 0.1 compare_select_fusion
  10.5 86.7 %scatter_custom_fusion = f32[786432]{0:T(1024)S(1)} fusion(s32[16384]{0:T(1024)S(1)} %bitcast.109, f32[16384]{0:T(1024)S(1)} %bitcast.108, f32[]{:T(128)} %constant.24.clone.1), kind=kCustom, calls=%fused_computation.45 | custom fusion | flops 16384 | bytes 3145732 | tf_op jit(solution)/shard_map/scatter-add | solution.py:29
  97.2 2.3 reshape.202
  99.5 0.0 copy-start
  99.5 0.0 copy-start.1
  99.5 0.0 copy-start.2
  99.5 6.1 %fusion.35 = (f32[512,1,2,512]{3,0,2,1:T(8,128)}, f32[1,512,2,512]{3,1,2,0:T(8,128)S(1)}, f32[1,512,2,512]{3,1,2,0:T(8,128)S(1)}, f32[512,1,2,512]{3,0,2,1:T(8,128)}) fusion(f32[512,1,512]{2,0,1:T(8,128)} %fusion.53, f32[512,1,512]{2,0,1:T(8,128)} %get-tuple-element.12, f32[512,1,512]{2,0,1:T(8,128)} %get-tuple-element.11), kind=kLoop, calls=%fused_computation.38 | loop fusion | flops 2097152 | bytes 11534336 | tf_op jit(solution)/shard_map/stack | solution.py:54
  105.6 0.0 copy-done
  105.6 0.0 copy-done.1
  105.6 0.0 copy-done.2
  105.6 10.1 %fusion.12 = f32[3,512,2,512]{1,3,2,0:T(8,128)S(1)} fusion(f32[3,512,512,1]{2,1,0,3:T(8,128)S(1)} %copy-done, f32[512,1,512]{2,0,1:T(8,128)S(1)} %copy-done.1, f32[512,1,512]{2,0,1:T(8,128)S(1)} %copy-done.2), kind=kOutput, calls=%fused_computation.19 | convolution fusion | flops 9664200704 | bytes 11534336 | tf_op jit(solution)/shard_map/zxy,yev->zxev/dot_general | solution.py:36
  115.8 22.1 %fusion.11 = bf16[3,2,512,512]{2,3,1,0:T(8,128)(2,1)} fusion(f32[1,512,2,512]{3,1,2,0:T(8,128)S(1)} %get-tuple-element.6, f32[1,512,2,512]{3,1,2,0:T(8,128)S(1)} %get-tuple-element.9, f32[3,512,2,512]{1,3,2,0:T(8,128)S(1)} %fusion.12), kind=kOutput, calls=%fused_computation.17 | convolution fusion | flops 19331547136 | bytes 13631488 | tf_op jit(solution)/shard_map/cuex,zxev->zcuv/dot_general | solution.py:41
  137.8 7.3 %copy.22 = bf16[3,2,512,512]{3,1,0,2:T(2,128)(2,1)S(1)} copy(bf16[3,2,512,512]{2,3,1,0:T(8,128)(2,1)} %fusion.11) | data formatting | bytes 6291456 | tf_op jit(solution)/shard_map/convert_element_type | solution.py:42
  145.2 53.2 %all_to_all.33 = bf16[3,2,512,512]{3,1,0,2:T(2,128)(2,1)S(1)} all-to-all(bf16[3,2,512,512]{3,1,0,2:T(2,128)(2,1)S(1)} %copy.22), channel_id=1, replica_groups=mesh['zg'=2,'xy'=64] {'zg','xy'}, dimensions={2} | all-to-all | bytes 6291456 | tf_op jit(solution)/shard_map/all_to_all | solution.py:43
  198.4 3.3 %copy.24 = bf16[128,3,2,4,512]{4,3,2,1,0:T(4,128)(2,1)} copy(bf16[128,3,2,4,512]{4,2,1,3,0:T(2,128)(2,1)S(1)} %bitcast.103) | data formatting | bytes 6291456 | tf_op jit(solution)/shard_map/all_to_all | solution.py:43
  201.6 4.0 %reshape.193 = bf16[384,2,4,4,128]{4,3,2,1,0:T(4,128)(2,1)S(1)} reshape(bf16[128,3,2,4,512]{4,3,2,1,0:T(4,128)(2,1)} %copy.24) | data formatting | bytes 6291456 | tf_op jit(solution)/shard_map/reshape | solution.py:45
  205.7 5.4 %convert_bitcast_fusion = bf16[384,2,4,4,128]{0,4,1,3,2:T(8,128)(2,1)S(1)} fusion(bf16[4,4,384,384]{3,2,1,0:T(8,128)(2,1)} %param.9, bf16[384,2,4,4,128]{4,3,2,1,0:T(4,128)(2,1)S(1)} %reshape.193), kind=kOutput, calls=%fused_computation.22 | convolution fusion | flops 1209532416 | bytes 11010048 | tf_op jit(solution)/shard_map/abzw,wcabj->zcabj/dot_general | solution.py:46
  211.1 0.4 copy.26
  211.5 4.4 %copy.27 = bf16[384,2,4,512]{3,2,1,0:T(4,128)(2,1)} copy(bf16[384,2,4,512]{0,3,2,1:T(8,128)(2,1)S(1)} %bitcast.104) | data formatting | bytes 6291456 | tf_op jit(solution)/shard_map/convert_element_type | solution.py:48
  215.8 4.8 %all-to-all-start.1 = ((bf16[384,2,4,512]{3,2,1,0:T(4,128)(2,1)}), bf16[384,2,4,512]{3,2,1,0:T(4,128)(2,1)S(1)}, u32[]{:S(2)}, u32[]{:S(2)}) async-start(bf16[384,2,4,512]{3,2,1,0:T(4,128)(2,1)} %copy.27), calls=%async_computation.1 | async-start | bytes 6291456 | tf_op jit(solution)/shard_map/all_to_all | solution.py:47
  220.6 5.0 %sine_negate_fusion = (f32[1,512,512]{2,1,0:T(8,128)}, f32[1,512,512]{2,1,0:T(8,128)}) fusion(), kind=kLoop, calls=%fused_computation.53 | loop fusion | flops 3932160 | bytes 2097152 | tf_op jit(solution)/shard_map/neg | solution.py:35
  225.6 36.8 %all-to-all-done.1 = bf16[384,2,4,512]{3,2,1,0:T(4,128)(2,1)S(1)} async-done(((bf16[384,2,4,512]{3,2,1,0:T(4,128)(2,1)}), bf16[384,2,4,512]{3,2,1,0:T(4,128)(2,1)S(1)}, u32[]{:S(2)}, u32[]{:S(2)}) %all-to-all-start.1) | async-done | bytes 3145760 | tf_op jit(solution)/shard_map/all_to_all | solution.py:47
  262.4 4.9 %copy.28 = bf16[3,2,128,4,512]{4,1,3,2,0:T(2,128)(2,1)} copy(bf16[3,2,128,4,512]{4,3,1,0,2:T(4,128)(2,1)S(1)} %bitcast.102) | data formatting | bytes 6291456 | tf_op jit(solution)/shard_map/all_to_all | solution.py:47
  267.3 7.0 %copy.37 = bf16[3,2,512,512,1]{2,3,1,4,0:T(8,128)(2,1)S(1)} copy(bf16[3,2,512,512,1]{3,1,2,0,4:T(2,128)(2,1)} %bitcast.105) | data formatting | bytes 6291456 | tf_op jit(solution)/shard_map/all_to_all | solution.py:47
  274.3 0.0 copy-start.5
  274.3 0.0 copy-start.6
  274.3 6.5 %fusion.22 = f32[3,512,512,2,1]{2,1,4,3,0:T(8,128)S(1)} fusion(bf16[3,2,512,512,1]{2,3,1,4,0:T(8,128)(2,1)S(1)} %copy.37, f32[512,1,2,512]{3,0,2,1:T(8,128)} %get-tuple-element.10, f32[512,1,2,512]{3,0,2,1:T(8,128)} %get-tuple-element.5), kind=kOutput, calls=%fused_computation.28 | convolution fusion | flops 3225419776 | bytes 13631488 | tf_op jit(solution)/shard_map/xceu,zeuv->zxcv/dot_general | solution.py:59
  280.8 0.0 copy-done.5
  280.8 0.0 copy-done.6
  280.8 0.0 copy-start.3
  280.9 0.0 copy-start.4
  280.9 3.5 %fusion.28 = f32[3,512,512,2,1]{2,1,4,3,0:T(8,128)S(1)} fusion(bf16[3,2,512,512,1]{2,3,1,4,0:T(8,128)(2,1)S(1)} %copy.37, f32[512,1,2,512]{3,0,2,1:T(8,128)S(1)} %copy-done.6, f32[512,1,2,512]{3,0,2,1:T(8,128)S(1)} %copy-done.5), kind=kOutput, calls=%fused_computation.33 | convolution fusion | flops 3226468352 | bytes 13631488 | tf_op jit(solution)/shard_map/xceu,zeuv->zxcv/dot_general | solution.py:60
  284.3 0.0 copy-done.3
  284.4 0.0 copy-done.4
  284.4 12.0 %bitcast_multiply_fusion.1 = f32[3,512,512]{2,1,0:T(8,128)} fusion(f32[1,512,512]{2,1,0:T(8,128)S(1)} %copy-done.3, f32[1,512,512]{2,1,0:T(8,128)S(1)} %copy-done.4, f32[3,512,512,2,1]{2,1,4,3,0:T(8,128)S(1)} %fusion.28, f32[3,512,512,2,1]{2,1,4,3,0:T(8,128)S(1)} %fusion.22), kind=kOutput, calls=%fused_computation.18 | convolution fusion | flops 9666560000 | bytes 17825792 | tf_op jit(solution)/shard_map/zxcv,cvy->zxy/dot_general | solution.py:65
  (3 shorter events, 0.0 us)
Async XLA Ops:
  0.0 10.2 %copy-start.9 = (f32[2048]{0:T(1024)S(1)}, f32[2048]{0:T(1024)}, u32[]{:S(2)}) copy-start(f32[2048]{0:T(1024)} %param.5) | copy-start | bytes 24580
  0.0 10.3 %copy-start.7 = (f32[8,2048]{1,0:T(8,128)S(1)}, f32[8,2048]{1,0:T(8,128)}, u32[]{:S(2)}) copy-start(f32[8,2048]{1,0:T(8,128)} %param.7) | copy-start | bytes 196612
  0.0 10.3 %copy-start.8 = (s32[8,2048]{1,0:T(8,128)S(1)}, s32[8,2048]{1,0:T(8,128)}, u32[]{:S(2)}) copy-start(s32[8,2048]{1,0:T(8,128)} %param.6) | copy-start | bytes 196612
  99.5 6.1 %copy-start = (f32[3,512,512,1]{2,1,0,3:T(8,128)S(1)}, f32[3,512,512,1]{2,1,0,3:T(8,128)}, u32[]{:S(2)}) copy-start(f32[3,512,512,1]{2,1,0,3:T(8,128)} %reshape.202) | copy-start | bytes 9437188
  99.5 6.1 %copy-start.1 = (f32[512,1,512]{2,0,1:T(8,128)S(1)}, f32[512,1,512]{2,0,1:T(8,128)}, u32[]{:S(2)}) copy-start(f32[512,1,512]{2,0,1:T(8,128)} %get-tuple-element.12) | copy-start | bytes 3145732
  99.5 6.1 %copy-start.2 = (f32[512,1,512]{2,0,1:T(8,128)S(1)}, f32[512,1,512]{2,0,1:T(8,128)}, u32[]{:S(2)}) copy-start(f32[512,1,512]{2,0,1:T(8,128)} %fusion.53) | copy-start | bytes 3145732
  215.8 46.5 %all-to-all-start.1 = ((bf16[384,2,4,512]{3,2,1,0:T(4,128)(2,1)}), bf16[384,2,4,512]{3,2,1,0:T(4,128)(2,1)S(1)}, u32[]{:S(2)}, u32[]{:S(2)}) async-start(bf16[384,2,4,512]{3,2,1,0:T(4,128)(2,1)} %copy.27), calls=%async_computation.1 | async-start | bytes 6291456 | tf_op jit(solution)/shard_map/all_to_all | solution.py:47
  274.3 6.5 %copy-start.5 = (f32[512,1,2,512]{3,0,2,1:T(8,128)S(1)}, f32[512,1,2,512]{3,0,2,1:T(8,128)}, u32[]{:S(2)}) copy-start(f32[512,1,2,512]{3,0,2,1:T(8,128)} %get-tuple-element.5) | copy-start | bytes 6291460
  274.3 6.5 %copy-start.6 = (f32[512,1,2,512]{3,0,2,1:T(8,128)S(1)}, f32[512,1,2,512]{3,0,2,1:T(8,128)}, u32[]{:S(2)}) copy-start(f32[512,1,2,512]{3,0,2,1:T(8,128)} %get-tuple-element.10) | copy-start | bytes 6291460
  280.8 3.5 %copy-start.3 = (f32[1,512,512]{2,1,0:T(8,128)S(1)}, f32[1,512,512]{2,1,0:T(8,128)}, u32[]{:S(2)}) copy-start(f32[1,512,512]{2,1,0:T(8,128)} %get-tuple-element.13) | copy-start | bytes 3145732
  280.9 3.5 %copy-start.4 = (f32[1,512,512]{2,1,0:T(8,128)S(1)}, f32[1,512,512]{2,1,0:T(8,128)}, u32[]{:S(2)}) copy-start(f32[1,512,512]{2,1,0:T(8,128)} %get-tuple-element.14) | copy-start | bytes 3145732
where the time goes:
time: 301 us; the launch traced here: 297 us
  other arithmetic  108 us (36%)
  matrix products  59.6 us (20%)
  blocking collectives  53.2 us (18%)
  waiting for transfers between devices  36.8 us (12%)
  local copies, waits for them, and re-layouts  33.7 us (11%)
  starting transfers between devices  4.78 us (2%)
    scatter-add x1, other arithmetic, shards(): jnp.zeros((slab * NX * NY,), jnp.float32).at[cells.reshape(-1)]  86.7 us
    all_to_all x1, blocking collectives, shards(): lax.all_to_all(spectrum, ('zg', 'xy'), split_axis=2, concat_axis=0, tiled...  53.2 us
    all_to_all x1, waiting for transfers between devices, shards(): lax.all_to_all(mixed.reshape(depth, parts, waves, width).astype(jnp.bfloa...  36.8 us
    dot_general x1, matrix products, shards(): jnp.einsum('cuex,zxev->zcuv', forward_x, along, precision=lax.Precision.H...  22.1 us
    dot_general x1, matrix products, shards(): jnp.einsum('zxcv,cvy->zxy', middle, inverse_y, precision=lax.Precision.HI...  12 us
    all_to_all x2, local copies, waits for them, and re-layouts, shards(): lax.all_to_all(mixed.reshape(depth, parts, waves, width).astype(jnp.bfloa...  11.9 us
    dot_general x1, matrix products, shards(): jnp.einsum('zxy,yev->zxev', density, forward_y, precision=lax.Precision.H...  10.1 us
    neg x2, other arithmetic, shards(): forward_y = jnp.stack([cos_y, -sin_y], axis=1)  9.62 us
  transfers between devices with their start and end apart: 1, of which 1 were waited for; matrix products, arithmetic and copies ran while one was open for 2% of the time, Pallas kernels for 0%

commit v1 on v0

v1 whole, which is shorter than its diff:
```python
import functools
import math

import numpy as np
import jax
import jax.numpy as jnp
from jax import lax
from jax.experimental import pallas as pl
from jax.experimental.pallas import tpu as pltpu
from jax.sharding import PartitionSpec as P

NX = 512
NY = 512
NZ = 384
HALF = 256
DEV = 128
SLAB = 3
SLOTS = 2048
SPREAD = 8
CHUNK = 256
CANDIDATES = 32
F32 = jnp.float32
BF16 = jnp.bfloat16


def split_table(table):
    high = table.astype(np.float32).astype(BF16)
    low = (table - high.astype(np.float64)).astype(np.float32).astype(BF16)
    return high, low


def make_tables():
    y = np.arange(NY)[:, None]
    v = np.arange(HALF)[None, :]
    angle = 2.0 * math.pi * (y * v % NY) / NY
    along_p = np.cos(angle)
    along_q = -np.sin(angle)
    along_q[:, 0] = 1.0 - 2.0 * (np.arange(NY) % 2)
    y_high, y_low = split_table(np.concatenate([along_p, along_q], axis=1))
    x = np.arange(HALF)[None, None, :]
    result = [y_high, y_low]
    for parity in range(2):
        u = (4 * np.arange(DEV)[:, None] + 2 * np.arange(2)[None, :] + parity)[:, :, None]
        angle = 2.0 * math.pi * (u * x % NX) / NX
        c, s = np.cos(angle), np.sin(angle)
        rows = [
            np.concatenate([c, s], axis=2),
            np.concatenate([-s, c], axis=2),
            np.concatenate([c, -s], axis=2),
            np.concatenate([-s, -c], axis=2),
        ]
        table = np.stack(rows, axis=1).reshape(DEV * 8, NX)
        result += split_table(table)
    return result


def make_shuffle():
    k, w = np.meshgrid(np.arange(16), np.arange(16), indexing="ij")
    shuffle = np.zeros((256, 256), np.float32)
    shuffle[(k * 16 + w).reshape(-1), (w * 16 + k).reshape(-1)] = 1.0
    return shuffle.astype(BF16)


def dot(a, b):
    return jnp.dot(a, b, preferred_element_type=F32)


def dot_nt(a, b):
    return lax.dot_general(a, b, (((1,), (1,)), ((), ())), preferred_element_type=F32)


def dot_tn(a, b):
    return lax.dot_general(a, b, (((0,), (0,)), ((), ())), preferred_element_type=F32)


def halves(value):
    high = value.astype(BF16)
    return high, (value - high.astype(F32)).astype(BF16)


def factor(value):
    best_left = jnp.ones_like(value)
    best_right = value.astype(BF16).astype(F32)
    best_error = jnp.abs(best_right - value)
    for j in range(1, CANDIDATES):
        left = 1.0 + j * (128 // CANDIDATES) / 128.0
        right = (value * (1.0 / left)).astype(BF16).astype(F32)
        error = jnp.abs(right * left - value)
        better = error < best_error
        best_error = jnp.where(better, error, best_error)
        best_right = jnp.where(better, right, best_right)
        best_left = jnp.where(better, left, best_left)
    return best_left, best_right


def prepare(counts, charges, splines, cells, left_ref, right_ref, row_ref, col_ref):
    slot = lax.broadcasted_iota(jnp.int32, (1, SLOTS), 1)
    live = jnp.where(slot < counts[0], charges[...], 0.0)
    left, right = factor(splines[...] * live)
    left_ref[...] = left
    right_ref[...] = right
    row_ref[...] = lax.shift_right_logical(cells[...], 9)
    col_ref[...] = lax.bitwise_and(cells[...], NY - 1)


def density_of(plane, left_ref, right_ref, row_ref, col_ref, total_ref):
    total_ref[...] = jnp.zeros_like(total_ref)
    index = lax.broadcasted_iota(jnp.int32, (NX, CHUNK), 0)
    index_row = index + plane * NX

    def body(c, carry):
        at = pl.ds(pl.multiple_of(c * CHUNK, CHUNK), CHUNK)
        a, b = [], []
        for k in range(SPREAD):
            a.append(jnp.where(row_ref[k : k + 1, at] == index_row, left_ref[k : k + 1, at], 0.0).astype(BF16))
            b.append(jnp.where(col_ref[k : k + 1, at] == index, right_ref[k : k + 1, at], 0.0).astype(BF16))
        total_ref[...] += dot_nt(jnp.concatenate(a, axis=1), jnp.concatenate(b, axis=1))
        return carry

    lax.fori_loop(0, SLOTS // CHUNK, body, 0)


def plane_spectrum(density, y_high, y_low, x_tables):
    high, low = halves(density)
    along = dot(high, y_high[...]) + dot(high, y_low[...]) + dot(low, y_high[...])
    folds = (along[:HALF] + along[HALF:], along[:HALF] - along[HALF:])
    parts = []
    for fold, (x_high, x_low) in zip(folds, x_tables):
        stacked = jnp.concatenate([fold[:, :HALF], fold[:, HALF:]], axis=0) * (1.0 / 512.0)
        high, low = halves(stacked)
        out = dot(x_high[...], high) + dot(x_high[...], low) + dot(x_low[...], high)
        parts.append(out.reshape(DEV, 8, HALF))
    return jnp.concatenate(parts, axis=1).astype(BF16)


def forward_kernel(
    counts, charges, splines, cells, y_high, y_low, even_high, even_low, odd_high, odd_low, out,
    left_ref, right_ref, row_ref, col_ref, total_ref,
):
    prepare(counts, charges, splines, cells, left_ref, right_ref, row_ref, col_ref)

    def plane_body(plane, carry):
        density_of(plane, left_ref, right_ref, row_ref, col_ref, total_ref)
        spectrum = plane_spectrum(
            total_ref[...], y_high, y_low, ((even_high, even_low), (odd_high, odd_low))
        )
        out[:, plane, 0] = spectrum[:, :, :128]
        out[:, plane, 1] = spectrum[:, :, 128:]
        return carry

    lax.fori_loop(0, SLAB, plane_body, 0)


def mix_kernel(green, shuffle, arrived, out, x_ref):
    first = lax.broadcasted_iota(jnp.int32, (NZ, 128), 1) == 0

    def turn(g, carry):
        at = pl.ds(g * 16, 16)
        block = jnp.concatenate(
            [arrived[at, 0].reshape(256, 128), arrived[at, 1].reshape(256, 128)], axis=1
        )
        x_ref[:, pl.ds(pl.multiple_of(g * 16, 16), 16), :] = (
            dot(shuffle[...], block).astype(BF16).reshape(16, 16, 256)
        )
        return carry

    lax.fori_loop(0, NZ // 16, turn, 0)

    def one_wave(parity, r):
        base = parity * 8 + r
        rows = [base, base + 2, base + 4, base + 6]
        pr, pi, mr, mi = (x_ref[row] for row in rows)
        p0 = [pr[:, :128].astype(F32), pi[:, :128].astype(F32)]
        m0 = [mr[:, :128].astype(F32), mi[:, :128].astype(F32)]
        m1 = [mr[:, 128:].astype(F32), mi[:, 128:].astype(F32)]
        zero = [(p0[0] + m0[0]) * 0.5, (p0[1] + m0[1]) * 0.5]
        last = [(p0[1] - m0[1]) * 0.5, (m0[0] - p0[0]) * 0.5]
        pick = lambda a, b: jnp.concatenate(
            [jnp.where(first, x, y) for x, y in zip(a, b)], axis=1
        ).astype(BF16)
        block0 = pick(zero, p0)
        block1 = jnp.concatenate([pr[:, 128:], pi[:, 128:]], axis=1)
        block2 = pick(last, m1)
        block3 = pick(m1, m0)
        u = 2 * r + parity
        y0, y1, y2, y3 = (
            dot(green[u, b], block) for b, block in enumerate((block0, block1, block2, block3))
        )
        re = lambda a: a[:, :128]
        im = lambda a: a[:, 128:]
        ar = jnp.where(first, (re(y0) - im(y2)) * 0.5, re(y0))
        ai = jnp.where(first, (im(y0) + re(y2)) * 0.5, im(y0))
        br = jnp.where(first, (re(y0) + im(y2)) * 0.5, re(y3))
        bi = jnp.where(first, (im(y0) - re(y2)) * 0.5, im(y3))
        cr = jnp.where(first, re(y3), re(y2))
        ci = jnp.where(first, im(y3), im(y2))
        x_ref[rows[0]] = jnp.concatenate([ar, re(y1)], axis=1).astype(BF16)
        x_ref[rows[1]] = jnp.concatenate([ai, im(y1)], axis=1).astype(BF16)
        x_ref[rows[2]] = jnp.concatenate([br, cr], axis=1).astype(BF16)
        x_ref[rows[3]] = jnp.concatenate([bi, ci], axis=1).astype(BF16)

    def wave_body(i, carry):
        one_wave(i // 2, i % 2)
        return carry

    lax.fori_loop(0, 4, wave_body, 0)

    def turn_back(g, carry):
        block = x_ref[:, pl.ds(pl.multiple_of(g * 16, 16), 16), :].reshape(256, 256)
        tiles = dot(shuffle[...], block).astype(BF16).reshape(16, 16, 256)
        at = pl.ds(g * 16, 16)
        out[at, 0] = tiles[:, :, :128]
        out[at, 1] = tiles[:, :, 128:]
        return carry

    lax.fori_loop(0, NZ // 16, turn_back, 0)


def inverse_kernel(arrived, y_high, even_high, odd_high, unzip, out, even_ref, odd_ref):
    even_t = even_high[...].T
    odd_t = odd_high[...].T

    def plane_body(plane, carry):
        def part(g, inner):
            at = pl.ds(g * 16, 16)
            block = jnp.concatenate(
                [arrived[at, plane, h].reshape(256, 128) for h in range(2)], axis=1
            )
            rows = dot(unzip[...], block).astype(BF16)
            to = pl.ds(pl.multiple_of(g * 128, 128), 128)
            even_ref[to, :] = rows[:128]
            odd_ref[to, :] = rows[128:]
            return inner

        lax.fori_loop(0, DEV // 16, part, 0)
        even = dot(even_t, even_ref[...])
        odd = dot(odd_t, odd_ref[...])
        lower, upper = even + odd, even - odd
        middle = jnp.concatenate(
            [
                jnp.concatenate([lower[:HALF], lower[HALF:]], axis=1),
                jnp.concatenate([upper[:HALF], upper[HALF:]], axis=1),
            ],
            axis=0,
        ).astype(BF16)
        out[plane] = dot_nt(middle, y_high[...]) * (1.0 / 512.0)
        return carry

    lax.fori_loop(0, SLAB, plane_body, 0)


def make_unzip():
    q, d, k = np.meshgrid(np.arange(2), np.arange(16), np.arange(8), indexing="ij")
    unzip = np.zeros((256, 256), np.float32)
    unzip[(q * 128 + d * 8 + k).reshape(-1), (d * 16 + q * 8 + k).reshape(-1)] = 1.0
    return unzip.astype(BF16)


VMEM = pl.BlockSpec(memory_space=pltpu.VMEM)
PARAMS = pltpu.CompilerParams(vmem_limit_bytes=60 * 2**20)


def shards(charges, cells, splines, counts, green):
    tables = make_tables()
    shuffle = make_shuffle()
    spectrum = pl.pallas_call(
        forward_kernel,
        out_shape=jax.ShapeDtypeStruct((DEV, SLAB, 2, 16, 128), BF16),
        in_specs=[pl.BlockSpec(memory_space=pltpu.SMEM)] + [VMEM] * 9,
        out_specs=VMEM,
        scratch_shapes=[
            pltpu.VMEM((SPREAD, SLOTS), F32),
            pltpu.VMEM((SPREAD, SLOTS), F32),
            pltpu.VMEM((SPREAD, SLOTS), jnp.int32),
            pltpu.VMEM((SPREAD, SLOTS), jnp.int32),
            pltpu.VMEM((NX, NY), F32),
        ],
        compiler_params=PARAMS,
        name="forward",
    )(counts, charges.reshape(1, SLOTS), splines, cells, *tables)
    arrived = lax.all_to_all(spectrum, ("zg", "xy"), split_axis=0, concat_axis=0, tiled=True)
    mixed = pl.pallas_call(
        mix_kernel,
        out_shape=jax.ShapeDtypeStruct((NZ, 2, 16, 128), BF16),
        in_specs=[VMEM] * 3,
        out_specs=VMEM,
        scratch_shapes=[pltpu.VMEM((16, NZ, 256), BF16)],
        compiler_params=PARAMS,
        name="mix",
    )(green, shuffle, arrived.reshape(NZ, 2, 16, 128))
    returned = lax.all_to_all(
        mixed.reshape(DEV, SLAB, 2, 16, 128), ("zg", "xy"), split_axis=0, concat_axis=0, tiled=True
    )
    return pl.pallas_call(
        inverse_kernel,
        out_shape=jax.ShapeDtypeStruct((SLAB, NX, NY), F32),
        in_specs=[VMEM] * 5,
        out_specs=VMEM,
        scratch_shapes=[pltpu.VMEM((DEV * 8, HALF), BF16), pltpu.VMEM((DEV * 8, HALF), BF16)],
        compiler_params=PARAMS,
        name="inverse",
    )(returned, tables[0], tables[2], tables[4], make_unzip())


def solution(mesh):
    in_specs = (
        P(("zg", "xy")),
        P(None, ("zg", "xy")),
        P(None, ("zg", "xy")),
        P(("zg", "xy")),
        P(("zg", "xy"), None, None, None),
    )
    out_specs = P(("zg", "xy"), None, None)
    return jax.shard_map(shards, mesh=mesh, in_specs=in_specs, out_specs=out_specs, check_vma=False)
```

time: 301 us -> 175 us (0.58); the launches traced: 297 us -> 175 us
  other arithmetic: 108 us -> 0 us
  Pallas kernels: 0 us -> 73.9 us
  matrix products: 59.6 us -> 0 us
  blocking collectives: 53.2 us -> 101 us
  waiting for transfers between devices: 36.8 us -> 0 us
  local copies, waits for them, and re-layouts: 33.7 us -> 0 us
  starting transfers between devices: 4.78 us -> 0 us
    scatter-add x1 -> x0, other arithmetic: 86.7 us -> none  [shards(): jnp.zeros((slab * NX * NY,), jnp.float32).at[cells.reshape(-1)]]
    pallas_call x0 -> x3, Pallas kernels: none -> 73.9 us  [the longest x1 44.6 us: shards(): pl.pallas_call(forward_kernel, out_shape=jax.ShapeDtypeStruct((DEV, SLAB,...]
    dot_general x6 -> x0, matrix products: 59.6 us -> none  [the longest x1 22.1 us: shards(): jnp.einsum('cuex,zxev->zcuv', forward_x, along, precision=lax.Precision.H...]
    all_to_all x1 -> x2, blocking collectives: 53.2 us -> 101 us  [the longest x1 53.4 us: shards(): lax.all_to_all(spectrum, ('zg', 'xy'), split_axis=0, concat_axis=0, tiled...]
    all_to_all x1 -> x0, waiting for transfers between devices: 36.8 us -> none  [shards(): lax.all_to_all(mixed.reshape(depth, parts, waves, width).astype(jnp.bfloa...]
    all_to_all x3 -> x0, local copies, waits for them, and re-layouts: 15.2 us -> none  [the longest x2 11.9 us: shards(): lax.all_to_all(mixed.reshape(depth, parts, waves, width).astype(jnp.bfloa...]
    convert_element_type x3 -> x0, local copies, waits for them, and re-layouts: 12.1 us -> none  [the longest x1 7.3 us: shards(): spectrum = (jnp.einsum('cuex,zxev->zcuv', forward_x, along, precision=lax...]
    neg x2 -> x0, other arithmetic: 9.62 us -> none  [shards(): forward_y = jnp.stack([cos_y, -sin_y], axis=1)]
  transfers between devices with their start and end apart: 1 -> 0, of which waited for: 1 -> 0; matrix products, arithmetic and copies ran while one was open for 2% -> 0% of each run, Pallas kernels for 0% -> 0%
where the time goes in v1:
time: 175 us
  blocking collectives  101 us (58%)
  Pallas kernels  73.9 us (42%)
    all_to_all x1, blocking collectives, shards(): lax.all_to_all(spectrum, ('zg', 'xy'), split_axis=0, concat_axis=0, tiled...  53.4 us
    all_to_all x1, blocking collectives, shards(): lax.all_to_all(mixed.reshape(DEV, SLAB, 2, 16, 128), ('zg', 'xy'), split_...  47.2 us
    pallas_call x1, Pallas kernels, shards(): pl.pallas_call(forward_kernel, out_shape=jax.ShapeDtypeStruct((DEV, SLAB,...  44.6 us
    pallas_call x1, Pallas kernels, shards(): pl.pallas_call(mix_kernel, out_shape=jax.ShapeDtypeStruct((NZ, 2, 16, 128...  16.8 us
    pallas_call x1, Pallas kernels, shards(): pl.pallas_call(inverse_kernel, out_shape=jax.ShapeDtypeStruct((SLAB, NX,...  12.5 us

profile of v1, /device:TPU:1, one launch (start us, length us, event | category | flops | bytes accessed | tf_op | source)
XLA Modules:
  0.0 175.1 jit_solution(16076208123681333217)
XLA Ops:
  0.7 44.6 %forward.1 = bf16[128,3,2,16,128]{4,3,2,1,0:T(8,128)(2,1)} custom-call(s32[1]{0:T(128)S(6)} %copy.14.counts, f32[1,2048]{1,0:T(1,128)} %bitcast.5, f32[8,2048]{1,0:T(8,128)} %splines.1, s32[8,2048]{1,0:T(8,128)} %cells.1, bf16[512,512]{1,0:T(8,128)(2,1)} %constant.16.clone.y_high, bf16[512,512]{1,0:T(8,128)(2,1)} %constant.17.clone.y_low, ...), custom_call_target="tpu_custom_call" | custom-call | tf_op jit(solution)/shard_map/forward/pallas_call | solution.py:266
  45.3 53.4 %all_to_all.10 = bf16[128,3,2,16,128]{4,3,2,1,0:T(8,128)(2,1)} all-to-all(bf16[128,3,2,16,128]{4,3,2,1,0:T(8,128)(2,1)} %forward.1), channel_id=1, replica_groups=mesh['zg'=2,'xy'=64] {'zg','xy'}, dimensions={0} | all-to-all | bytes 6291456 | tf_op jit(solution)/shard_map/all_to_all | solution.py:281
  98.6 16.8 %mix.1 = bf16[384,2,16,128]{3,2,1,0:T(8,128)(2,1)} custom-call(bf16[4,4,384,384]{3,2,1,0:T(8,128)(2,1)} %green.1, bf16[256,256]{1,0:T(8,128)(2,1)} %constant.22.clone.shuffle, bf16[384,2,16,128]{3,2,1,0:T(8,128)(2,1)} %bitcast.3), custom_call_target="tpu_custom_call" | custom-call | tf_op jit(solution)/shard_map/mix/pallas_call | solution.py:282
  115.4 47.2 %all_to_all.11.arrived = bf16[128,3,2,16,128]{4,3,2,1,0:T(8,128)(2,1)} all-to-all(bf16[128,3,2,16,128]{4,3,2,1,0:T(8,128)(2,1)} %bitcast.4), channel_id=1, replica_groups=mesh['zg'=2,'xy'=64] {'zg','xy'}, dimensions={0} | all-to-all | bytes 6291456 | tf_op jit(solution)/shard_map/all_to_all | solution.py:291
  162.6 12.5 %inverse.1 = f32[3,512,512]{2,1,0:T(8,128)} custom-call(bf16[128,3,2,16,128]{4,3,2,1,0:T(8,128)(2,1)} %all_to_all.11.arrived, bf16[512,512]{1,0:T(8,128)(2,1)} %constant.16.clone.y_high, bf16[1024,512]{1,0:T(8,128)(2,1)} %constant.18.clone.even_high, bf16[1024,512]{1,0:T(8,128)(2,1)} %constant.20.clone.odd_high, bf16[256,256]{1,0:T(8,128)(2,1)} %constant.23.clone.unzip), custom_call_target="tpu_custom_call" | custom-call | tf_op jit(solution)/shard_map/inverse/pallas_call | solution.py:294

commit v2 on v1

--- a/solution.py
+++ b/solution.py
@@ -19,6 +19,7 @@
 SPREAD = 8
 CHUNK = 256
 CANDIDATES = 32
+STEP = 37
 F32 = jnp.float32
 BF16 = jnp.bfloat16
 
@@ -133,38 +134,135 @@
     return jnp.concatenate(parts, axis=1).astype(BF16)
 
 
-def forward_kernel(
-    counts, charges, splines, cells, y_high, y_low, even_high, even_low, odd_high, odd_low, out,
-    left_ref, right_ref, row_ref, col_ref, total_ref,
+def make_unzip():
+    q, d, k = np.meshgrid(np.arange(2), np.arange(16), np.arange(8), indexing="ij")
+    unzip = np.zeros((256, 256), np.float32)
+    unzip[(q * 128 + d * 8 + k).reshape(-1), (d * 16 + q * 8 + k).reshape(-1)] = 1.0
+    return unzip.astype(BF16)
+
+
+def peer_of(me, i):
+    return lax.rem(me + STEP * i, DEV)
+
+
+def place(device):
+    return (device // 64, lax.rem(device, 64))
+
+
+def fused_kernel(
+    counts, charges, splines, cells, shuffle, unzip, *rest,
 ):
+    sources, middle = rest[:7], rest[7]
+    left_ref, right_ref, row_ref, col_ref, total_ref = rest[8:13]
+    held, (green,) = rest[13:19], rest[19:20]
+    send1, arrive1, x_ref, send2, arrive2, even_ref, odd_ref, even_t, odd_t = rest[20:29]
+    load_sem, send_sem, arrive1_sem, arrive2_sem = rest[29:33]
+    y_high, y_low, even_high, even_low, odd_high, odd_low = held
+    me = lax.axis_index("zg") * 64 + lax.axis_index("xy")
+
+    barrier = pltpu.get_barrier_semaphore()
+
+    def greet(i, carry):
+        pl.semaphore_signal(
+            barrier, inc=1, device_id=place(peer_of(me, i)), device_id_type=pl.DeviceIdType.MESH
+        )
+        return carry
+
+    lax.fori_loop(1, DEV, greet, 0)
+    loads = [
+        pltpu.make_async_copy(source, target, load_sem.at[i])
+        for i, (source, target) in enumerate(zip(sources, (*held, green)))
+    ]
+    for load in loads:
+        load.start()
     prepare(counts, charges, splines, cells, left_ref, right_ref, row_ref, col_ref)
 
     def plane_body(plane, carry):
         density_of(plane, left_ref, right_ref, row_ref, col_ref, total_ref)
+
+        @pl.when(plane == 0)
+        def _():
+            for load in loads[:6]:
+                load.wait()
+            pl.semaphore_wait(barrier, DEV - 1)
+
         spectrum = plane_spectrum(
             total_ref[...], y_high, y_low, ((even_high, even_low), (odd_high, odd_low))
         )
-        out[:, plane, 0] = spectrum[:, :, :128]
-        out[:, plane, 1] = spectrum[:, :, 128:]
+        send1[plane, :, 0] = spectrum[:, :, :128]
+        send1[plane, :, 1] = spectrum[:, :, 128:]
+
+        def send(i, inner):
+            peer = peer_of(me, i)
+            pltpu.make_async_remote_copy(
+                src_ref=send1.at[plane, peer],
+                dst_ref=arrive1.at[me, plane],
+                send_sem=send_sem.at[0],
+                recv_sem=arrive1_sem,
+                device_id=place(peer),
+                device_id_type=pl.DeviceIdType.MESH,
+            ).start()
+            return inner
+
+        lax.fori_loop(1, DEV, send, 0)
+        arrive1[me, plane] = send1[plane, me]
         return carry
 
     lax.fori_loop(0, SLAB, plane_body, 0)
-
-
-def mix_kernel(green, shuffle, arrived, out, x_ref):
+    even_t[...] = even_high[...].T
+    odd_t[...] = odd_high[...].T
+    loads[6].wait()
+    most = arrive1.at[pl.ds(0, DEV - 1)]
+    pltpu.make_async_copy(most, most, arrive1_sem).wait()
+
+    mix(green, shuffle, arrive1, send2, x_ref)
+
+    for plane in range(SLAB):
+
+        def send(i, inner):
+            peer = peer_of(me, i)
+            pltpu.make_async_remote_copy(
+                src_ref=send2.at[peer, plane],
+                dst_ref=arrive2.at[plane, me],
+                send_sem=send_sem.at[1],
+                recv_sem=arrive2_sem.at[plane],
+                device_id=place(peer),
+                device_id_type=pl.DeviceIdType.MESH,
+            ).start()
+            return inner
+
+        lax.fori_loop(1, DEV, send, 0)
+        arrive2[plane, me] = send2[me, plane]
+
+    for plane in range(SLAB):
+        most = arrive2.at[plane, pl.ds(0, DEV - 1)]
+        pltpu.make_async_copy(most, most, arrive2_sem.at[plane]).wait()
+        middle[plane] = back_along_x(arrive2, plane, unzip, even_t, odd_t, even_ref, odd_ref)
+
+    most = arrive1.at[pl.ds(0, DEV - 1)]
+    for i in range(2):
+        pltpu.make_async_copy(most, most, send_sem.at[i]).wait()
+
+
+def mix(green, shuffle, arrived, out, x_ref):
     first = lax.broadcasted_iota(jnp.int32, (NZ, 128), 1) == 0
 
     def turn(g, carry):
         at = pl.ds(g * 16, 16)
-        block = jnp.concatenate(
-            [arrived[at, 0].reshape(256, 128), arrived[at, 1].reshape(256, 128)], axis=1
-        )
-        x_ref[:, pl.ds(pl.multiple_of(g * 16, 16), 16), :] = (
-            dot(shuffle[...], block).astype(BF16).reshape(16, 16, 256)
-        )
-        return carry
-
-    lax.fori_loop(0, NZ // 16, turn, 0)
+        for j in range(3):
+            block = jnp.concatenate(
+                [
+                    arrived[at, :, h].reshape(48, 16, 128)[16 * j : 16 * j + 16].reshape(256, 128)
+                    for h in range(2)
+                ],
+                axis=1,
+            )
+            x_ref[:, pl.ds(pl.multiple_of(g * 48 + j * 16, 16), 16), :] = (
+                dot(shuffle[...], block).astype(BF16).reshape(16, 16, 256)
+            )
+        return carry
+
+    lax.fori_loop(0, DEV // 16, turn, 0)
 
     def one_wave(parity, r):
         base = parity * 8 + r
@@ -206,67 +304,59 @@
     lax.fori_loop(0, 4, wave_body, 0)
 
     def turn_back(g, carry):
-        block = x_ref[:, pl.ds(pl.multiple_of(g * 16, 16), 16), :].reshape(256, 256)
-        tiles = dot(shuffle[...], block).astype(BF16).reshape(16, 16, 256)
+        tiles = []
+        for j in range(3):
+            block = x_ref[:, pl.ds(pl.multiple_of(g * 48 + j * 16, 16), 16), :].reshape(256, 256)
+            tiles.append(dot(shuffle[...], block).astype(BF16).reshape(16, 16, 256))
+        tiles = jnp.concatenate(tiles, axis=0).reshape(16, SLAB, 16, 256)
         at = pl.ds(g * 16, 16)
-        out[at, 0] = tiles[:, :, :128]
-        out[at, 1] = tiles[:, :, 128:]
-        return carry
-
-    lax.fori_loop(0, NZ // 16, turn_back, 0)
-
-
-def inverse_kernel(arrived, y_high, even_high, odd_high, unzip, out, even_ref, odd_ref):
-    even_t = even_high[...].T
-    odd_t = odd_high[...].T
-
-    def plane_body(plane, carry):
-        def part(g, inner):
-            at = pl.ds(g * 16, 16)
+        out[at, :, 0] = tiles[..., :128]
+        out[at, :, 1] = tiles[..., 128:]
+        return carry
+
+    lax.fori_loop(0, DEV // 16, turn_back, 0)
+
+
+def back_along_x(arrived, plane, unzip, even_t, odd_t, even_ref, odd_ref):
+    def part(g, inner):
+        for j in range(2):
+            at = pl.ds(g * 32 + j * 16, 16)
             block = jnp.concatenate(
-                [arrived[at, plane, h].reshape(256, 128) for h in range(2)], axis=1
+                [arrived[plane, at, h].reshape(256, 128) for h in range(2)], axis=1
             )
             rows = dot(unzip[...], block).astype(BF16)
-            to = pl.ds(pl.multiple_of(g * 128, 128), 128)
+            to = pl.ds(pl.multiple_of(g * 256 + j * 128, 128), 128)
             even_ref[to, :] = rows[:128]
             odd_ref[to, :] = rows[128:]
-            return inner
-
-        lax.fori_loop(0, DEV // 16, part, 0)
-        even = dot(even_t, even_ref[...])
-        odd = dot(odd_t, odd_ref[...])
-        lower, upper = even + odd, even - odd
-        middle = jnp.concatenate(
-            [
-                jnp.concatenate([lower[:HALF], lower[HALF:]], axis=1),
-                jnp.concatenate([upper[:HALF], upper[HALF:]], axis=1),
-            ],
-            axis=0,
-        ).astype(BF16)
-        out[plane] = dot_nt(middle, y_high[...]) * (1.0 / 512.0)
-        return carry
-
-    lax.fori_loop(0, SLAB, plane_body, 0)
-
-
-def make_unzip():
-    q, d, k = np.meshgrid(np.arange(2), np.arange(16), np.arange(8), indexing="ij")
-    unzip = np.zeros((256, 256), np.float32)
-    unzip[(q * 128 + d * 8 + k).reshape(-1), (d * 16 + q * 8 + k).reshape(-1)] = 1.0
-    return unzip.astype(BF16)
+        return inner
+
+    lax.fori_loop(0, DEV // 32, part, 0)
+    even = dot(even_t[...], even_ref[...])
+    odd = dot(odd_t[...], odd_ref[...])
+    lower, upper = even + odd, even - odd
+    return jnp.concatenate(
+        [
+            jnp.concatenate([lower[:HALF], lower[HALF:]], axis=1),
+            jnp.concatenate([upper[:HALF], upper[HALF:]], axis=1),
+        ],
+        axis=0,
+    ).astype(BF16)
+
+
+def back_along_y(middle, y_high, out):
+    out[0] = dot_nt(middle[0], y_high[...]) * (1.0 / 512.0)
 
 
 VMEM = pl.BlockSpec(memory_space=pltpu.VMEM)
-PARAMS = pltpu.CompilerParams(vmem_limit_bytes=60 * 2**20)
+ANY = pl.BlockSpec(memory_space=pl.ANY)
 
 
 def shards(charges, cells, splines, counts, green):
     tables = make_tables()
-    shuffle = make_shuffle()
-    spectrum = pl.pallas_call(
-        forward_kernel,
-        out_shape=jax.ShapeDtypeStruct((DEV, SLAB, 2, 16, 128), BF16),
-        in_specs=[pl.BlockSpec(memory_space=pltpu.SMEM)] + [VMEM] * 9,
+    middle = pl.pallas_call(
+        fused_kernel,
+        out_shape=jax.ShapeDtypeStruct((SLAB, NX, NY), BF16),
+        in_specs=[pl.BlockSpec(memory_space=pltpu.SMEM)] + [VMEM] * 5 + [ANY] * 7,
         out_specs=VMEM,
         scratch_shapes=[
             pltpu.VMEM((SPREAD, SLOTS), F32),
@@ -274,32 +364,38 @@
             pltpu.VMEM((SPREAD, SLOTS), jnp.int32),
             pltpu.VMEM((SPREAD, SLOTS), jnp.int32),
             pltpu.VMEM((NX, NY), F32),
+            *[pltpu.VMEM(table.shape, BF16) for table in tables],
+            pltpu.VMEM(green.shape, BF16),
+            pltpu.VMEM((SLAB, DEV, 2, 16, 128), BF16),
+            pltpu.VMEM((DEV, SLAB, 2, 16, 128), BF16),
+            pltpu.VMEM((16, NZ, 256), BF16),
+            pltpu.VMEM((DEV, SLAB, 2, 16, 128), BF16),
+            pltpu.VMEM((SLAB, DEV, 2, 16, 128), BF16),
+            pltpu.VMEM((DEV * 8, HALF), BF16),
+            pltpu.VMEM((DEV * 8, HALF), BF16),
+            pltpu.VMEM((NX, DEV * 8), BF16),
+            pltpu.VMEM((NX, DEV * 8), BF16),
+            pltpu.SemaphoreType.DMA((7,)),
+            pltpu.SemaphoreType.DMA((2,)),
+            pltpu.SemaphoreType.DMA,
+            pltpu.SemaphoreType.DMA((SLAB,)),
         ],
-        compiler_params=PARAMS,
-        name="forward",
-    )(counts, charges.reshape(1, SLOTS), splines, cells, *tables)
-    arrived = lax.all_to_all(spectrum, ("zg", "xy"), split_axis=0, concat_axis=0, tiled=True)
-    mixed = pl.pallas_call(
-        mix_kernel,
-        out_shape=jax.ShapeDtypeStruct((NZ, 2, 16, 128), BF16),
-        in_specs=[VMEM] * 3,
-        out_specs=VMEM,
-        scratch_shapes=[pltpu.VMEM((16, NZ, 256), BF16)],
-        compiler_params=PARAMS,
-        name="mix",
-    )(green, shuffle, arrived.reshape(NZ, 2, 16, 128))
-    returned = lax.all_to_all(
-        mixed.reshape(DEV, SLAB, 2, 16, 128), ("zg", "xy"), split_axis=0, concat_axis=0, tiled=True
-    )
+        compiler_params=pltpu.CompilerParams(
+            collective_id=0, has_side_effects=True, vmem_limit_bytes=60 * 2**20
+        ),
+        name="fused",
+    )(counts, charges.reshape(1, SLOTS), splines, cells, make_shuffle(), make_unzip(), *tables, green)
     return pl.pallas_call(
-        inverse_kernel,
+        back_along_y,
+        grid=(SLAB,),
         out_shape=jax.ShapeDtypeStruct((SLAB, NX, NY), F32),
-        in_specs=[VMEM] * 5,
-        out_specs=VMEM,
-        scratch_shapes=[pltpu.VMEM((DEV * 8, HALF), BF16), pltpu.VMEM((DEV * 8, HALF), BF16)],
-        compiler_params=PARAMS,
-        name="inverse",
-    )(returned, tables[0], tables[2], tables[4], make_unzip())
+        in_specs=[
+            pl.BlockSpec((1, NX, NY), lambda i: (i, 0, 0)),
+            pl.BlockSpec((NY, NY), lambda i: (0, 0)),
+        ],
+        out_specs=pl.BlockSpec((1, NX, NY), lambda i: (i, 0, 0)),
+        name="back_along_y",
+    )(middle, tables[0])
 
 
 def solution(mesh):

time: 175 us -> 122 us (0.70)
  blocking collectives: 101 us -> 0 us
  Pallas kernels: 73.9 us -> 121 us
    all_to_all x2 -> x0, blocking collectives: 101 us -> none  [the longest x1 53.4 us: shards(): lax.all_to_all(spectrum, ('zg', 'xy'), split_axis=0, concat_axis=0, tiled...]
    pallas_call x3 -> x2, Pallas kernels: 73.9 us -> 121 us  [the longest x1 116 us: shards(): pl.pallas_call(fused_kernel, out_shape=jax.ShapeDtypeStruct((SLAB, NX, NY...]
where the time goes in v2:
time: 122 us
  Pallas kernels  121 us (99%)
    pallas_call x1, Pallas kernels, shards(): pl.pallas_call(fused_kernel, out_shape=jax.ShapeDtypeStruct((SLAB, NX, NY...  116 us
    pallas_call x1, Pallas kernels, shards(): pl.pallas_call(back_along_y, grid=(SLAB,), out_shape=jax.ShapeDtypeStruct...  4.56 us

profile of v2, /device:TPU:1, one launch (start us, length us, event | category | flops | bytes accessed | tf_op | source)
XLA Modules:
  0.0 121.6 jit_solution(10430698901455805037)
XLA Ops:
  0.7 116.4 %fused.1.middle = bf16[3,512,512]{2,1,0:T(8,128)(2,1)} custom-call(s32[1]{0:T(128)S(6)} %copy.14.counts, f32[1,2048]{1,0:T(1,128)} %bitcast.1, f32[8,2048]{1,0:T(8,128)} %splines.1, s32[8,2048]{1,0:T(8,128)} %cells.1, bf16[256,256]{1,0:T(8,128)(2,1)} %constant.16.clone.shuffle, bf16[256,256]{1,0:T(8,128)(2,1)} %constant.17.clone.unzip, ...), custom_call_target="tpu_custom_call" | custom-call | tf_op jit(solution)/shard_map/fused/pallas_call | solution.py:356
  117.1 4.6 %back_along_y.1 = f32[3,512,512]{2,1,0:T(8,128)} custom-call(bf16[3,512,512]{2,1,0:T(8,128)(2,1)} %fused.1.middle, bf16[512,512]{1,0:T(8,128)(2,1)} %constant.18.clone.rest_0_.y_high), custom_call_target="tpu_custom_call" | custom-call | tf_op jit(solution)/shard_map/back_along_y/pallas_call | solution.py:388

commit v3 on v2

--- a/solution.py
+++ b/solution.py
@@ -17,9 +17,10 @@
 SLAB = 3
 SLOTS = 2048
 SPREAD = 8
-CHUNK = 256
+CHUNK = 1024
 CANDIDATES = 32
 STEP = 37
+GROUP = 9
 F32 = jnp.float32
 BF16 = jnp.bfloat16
 
@@ -145,6 +146,16 @@
     return lax.rem(me + STEP * i, DEV)
 
 
+def each_peer(me, action):
+    def several(j, carry):
+        for k in range(GROUP):
+            action(peer_of(me, 1 + GROUP * j + k))
+        return carry
+
+    lax.fori_loop(0, (DEV - 2) // GROUP, several, 0)
+    action(peer_of(me, DEV - 1))
+
+
 def place(device):
     return (device // 64, lax.rem(device, 64))
 
@@ -162,19 +173,18 @@
 
     barrier = pltpu.get_barrier_semaphore()
 
-    def greet(i, carry):
+    def greet(peer):
         pl.semaphore_signal(
-            barrier, inc=1, device_id=place(peer_of(me, i)), device_id_type=pl.DeviceIdType.MESH
+            barrier, inc=1, device_id=place(peer), device_id_type=pl.DeviceIdType.MESH
         )
-        return carry
-
-    lax.fori_loop(1, DEV, greet, 0)
+
     loads = [
         pltpu.make_async_copy(source, target, load_sem.at[i])
         for i, (source, target) in enumerate(zip(sources, (*held, green)))
     ]
     for load in loads:
         load.start()
+    each_peer(me, greet)
     prepare(counts, charges, splines, cells, left_ref, right_ref, row_ref, col_ref)
 
     def plane_body(plane, carry):
@@ -192,8 +202,7 @@
         send1[plane, :, 0] = spectrum[:, :, :128]
         send1[plane, :, 1] = spectrum[:, :, 128:]
 
-        def send(i, inner):
-            peer = peer_of(me, i)
+        def send(peer):
             pltpu.make_async_remote_copy(
                 src_ref=send1.at[plane, peer],
                 dst_ref=arrive1.at[me, plane],
@@ -202,9 +211,8 @@
                 device_id=place(peer),
                 device_id_type=pl.DeviceIdType.MESH,
             ).start()
-            return inner
-
-        lax.fori_loop(1, DEV, send, 0)
+
+        each_peer(me, send)
         arrive1[me, plane] = send1[plane, me]
         return carry
 
@@ -219,8 +227,7 @@
 
     for plane in range(SLAB):
 
-        def send(i, inner):
-            peer = peer_of(me, i)
+        def send(peer):
             pltpu.make_async_remote_copy(
                 src_ref=send2.at[peer, plane],
                 dst_ref=arrive2.at[plane, me],
@@ -229,9 +236,8 @@
                 device_id=place(peer),
                 device_id_type=pl.DeviceIdType.MESH,
             ).start()
-            return inner
-
-        lax.fori_loop(1, DEV, send, 0)
+
+        each_peer(me, send)
         arrive2[plane, me] = send2[me, plane]
 
     for plane in range(SLAB):
@@ -262,7 +268,7 @@
             )
         return carry
 
-    lax.fori_loop(0, DEV // 16, turn, 0)
+    lax.fori_loop(0, DEV // 16, turn, 0, unroll=8)
 
     def one_wave(parity, r):
         base = parity * 8 + r
@@ -301,7 +307,7 @@
         one_wave(i // 2, i % 2)
         return carry
 
-    lax.fori_loop(0, 4, wave_body, 0)
+    lax.fori_loop(0, 4, wave_body, 0, unroll=4)
 
     def turn_back(g, carry):
         tiles = []
@@ -314,7 +320,7 @@
         out[at, :, 1] = tiles[..., 128:]
         return carry
 
-    lax.fori_loop(0, DEV // 16, turn_back, 0)
+    lax.fori_loop(0, DEV // 16, turn_back, 0, unroll=8)
 
 
 def back_along_x(arrived, plane, unzip, even_t, odd_t, even_ref, odd_ref):
@@ -330,7 +336,7 @@
             odd_ref[to, :] = rows[128:]
         return inner
 
-    lax.fori_loop(0, DEV // 32, part, 0)
+    lax.fori_loop(0, DEV // 32, part, 0, unroll=4)
     even = dot(even_t[...], even_ref[...])
     odd = dot(odd_t[...], odd_ref[...])
     lower, upper = even + odd, even - odd

time: 122 us -> 112 us (0.918)
  Pallas kernels: 121 us -> 111 us
    pallas_call x1, Pallas kernels: 116 us -> 106 us  [shards(): pl.pallas_call(fused_kernel, out_shape=jax.ShapeDtypeStruct((SLAB, NX, NY...]
where the time goes in v3:
time: 112 us; the launch traced here: 111 us
  Pallas kernels  111 us (99%)
    pallas_call x1, Pallas kernels, shards(): pl.pallas_call(fused_kernel, out_shape=jax.ShapeDtypeStruct((SLAB, NX, NY...  106 us
    pallas_call x1, Pallas kernels, shards(): pl.pallas_call(back_along_y, grid=(SLAB,), out_shape=jax.ShapeDtypeStruct...  4.56 us

profile of v3, /device:TPU:1, one launch (start us, length us, event | category | flops | bytes accessed | tf_op | source)
XLA Modules:
  0.0 111.4 jit_solution(10214468150583584363)
XLA Ops:
  0.7 106.2 %fused.1.middle = bf16[3,512,512]{2,1,0:T(8,128)(2,1)} custom-call(s32[1]{0:T(128)S(6)} %copy.14.counts, f32[1,2048]{1,0:T(1,128)} %bitcast.1, f32[8,2048]{1,0:T(8,128)} %splines.1, s32[8,2048]{1,0:T(8,128)} %cells.1, bf16[256,256]{1,0:T(8,128)(2,1)} %constant.16.clone.shuffle, bf16[256,256]{1,0:T(8,128)(2,1)} %constant.17.clone.unzip, ...), custom_call_target="tpu_custom_call" | custom-call | tf_op jit(solution)/shard_map/fused/pallas_call | solution.py:362
  106.8 4.6 %back_along_y.1 = f32[3,512,512]{2,1,0:T(8,128)} custom-call(bf16[3,512,512]{2,1,0:T(8,128)(2,1)} %fused.1.middle, bf16[512,512]{1,0:T(8,128)(2,1)} %constant.18.clone.rest_0_.y_high), custom_call_target="tpu_custom_call" | custom-call | tf_op jit(solution)/shard_map/back_along_y/pallas_call | solution.py:394

commit v4 on v3

v4 whole, which is shorter than its diff:
```python
import functools
import math

import numpy as np
import jax
import jax.numpy as jnp
from jax import lax
from jax.experimental import pallas as pl
from jax.experimental.pallas import tpu as pltpu
from jax.sharding import PartitionSpec as P

NX = 512
NY = 512
NZ = 384
HALF = 256
DEV = 128
SLAB = 3
SLOTS = 2048
SPREAD = 8
CHUNK = 1024
CANDIDATES = 32
STEP = 37
GROUP = 9
F32 = jnp.float32
BF16 = jnp.bfloat16


def split_table(table):
    high = table.astype(np.float32).astype(BF16)
    low = (table - high.astype(np.float64)).astype(np.float32).astype(BF16)
    return high, low


def make_tables():
    y = np.arange(NY)[:, None]
    v = np.arange(HALF)[None, :]
    angle = 2.0 * math.pi * (y * v % NY) / NY
    along_p = np.cos(angle)
    along_q = -np.sin(angle)
    along_q[:, 0] = 1.0 - 2.0 * (np.arange(NY) % 2)
    y_high, y_low = split_table(np.concatenate([along_p, along_q], axis=1))
    x = np.arange(HALF)[None, None, :]
    result = [y_high, y_low]
    for parity in range(2):
        u = (4 * np.arange(DEV)[:, None] + 2 * np.arange(2)[None, :] + parity)[:, :, None]
        angle = 2.0 * math.pi * (u * x % NX) / NX
        c, s = np.cos(angle), np.sin(angle)
        rows = [
            np.concatenate([c, s], axis=2),
            np.concatenate([-s, c], axis=2),
            np.concatenate([c, -s], axis=2),
            np.concatenate([-s, -c], axis=2),
        ]
        table = np.stack(rows, axis=1).reshape(DEV * 8, NX)
        result += split_table(table)
    return result


def make_shuffle():
    k, w = np.meshgrid(np.arange(16), np.arange(16), indexing="ij")
    shuffle = np.zeros((256, 256), np.float32)
    shuffle[(k * 16 + w).reshape(-1), (w * 16 + k).reshape(-1)] = 1.0
    return shuffle.astype(BF16)


def dot(a, b):
    return jnp.dot(a, b, preferred_element_type=F32)


def dot_nt(a, b):
    return lax.dot_general(a, b, (((1,), (1,)), ((), ())), preferred_element_type=F32)


def dot_tn(a, b):
    return lax.dot_general(a, b, (((0,), (0,)), ((), ())), preferred_element_type=F32)


def halves(value):
    high = value.astype(BF16)
    return high, (value - high.astype(F32)).astype(BF16)


def factor(value):
    best_left = jnp.ones_like(value)
    best_right = value.astype(BF16).astype(F32)
    best_error = jnp.abs(best_right - value)
    for j in range(1, CANDIDATES):
        left = 1.0 + j * (128 // CANDIDATES) / 128.0
        right = (value * (1.0 / left)).astype(BF16).astype(F32)
        error = jnp.abs(right * left - value)
        better = error < best_error
        best_error = jnp.where(better, error, best_error)
        best_right = jnp.where(better, right, best_right)
        best_left = jnp.where(better, left, best_left)
    return best_left, best_right


def prepare(counts, charges, splines, cells, left_ref, right_ref, row_ref, col_ref):
    slot = lax.broadcasted_iota(jnp.int32, (1, SLOTS), 1)
    live = jnp.where(slot < counts[0], charges[...], 0.0)
    left, right = factor(splines[...] * live)
    left_ref[...] = left
    right_ref[...] = right
    row_ref[...] = lax.shift_right_logical(cells[...], 9)
    col_ref[...] = lax.bitwise_and(cells[...], NY - 1)


def density_of(plane, left_ref, right_ref, row_ref, col_ref, total_ref):
    total_ref[...] = jnp.zeros_like(total_ref)
    index = lax.broadcasted_iota(jnp.int32, (NX, CHUNK), 0)
    index_row = index + plane * NX

    def body(c, carry):
        at = pl.ds(pl.multiple_of(c * CHUNK, CHUNK), CHUNK)
        a, b = [], []
        for k in range(SPREAD):
            a.append(jnp.where(row_ref[k : k + 1, at] == index_row, left_ref[k : k + 1, at], 0.0).astype(BF16))
            b.append(jnp.where(col_ref[k : k + 1, at] == index, right_ref[k : k + 1, at], 0.0).astype(BF16))
        total_ref[...] += dot_nt(jnp.concatenate(a, axis=1), jnp.concatenate(b, axis=1))
        return carry

    lax.fori_loop(0, SLOTS // CHUNK, body, 0)


def along_y(density, y_high, y_low):
    high, low = halves(density)
    along = dot(high, y_high[...]) + dot(high, y_low[...]) + dot(low, y_high[...])
    return along[:HALF] + along[HALF:], along[:HALF] - along[HALF:]


def along_x(fold, x_high, x_low):
    stacked = jnp.concatenate([fold[:, :HALF], fold[:, HALF:]], axis=0) * (1.0 / 512.0)
    high, low = halves(stacked)
    out = dot(x_high[...], high) + dot(x_high[...], low) + dot(x_low[...], high)
    out = out.reshape(DEV, 8, HALF)
    return jnp.concatenate([out[:, :, :128], out[:, :, 128:]], axis=1).astype(BF16)


def make_unzip():
    q, d, k = np.meshgrid(np.arange(2), np.arange(16), np.arange(8), indexing="ij")
    unzip = np.zeros((256, 256), np.float32)
    unzip[(q * 128 + d * 8 + k).reshape(-1), (d * 16 + q * 8 + k).reshape(-1)] = 1.0
    return unzip.astype(BF16)


def peer_of(me, i):
    return lax.rem(me + STEP * i, DEV)


def each_peer(me, action):
    def several(j, carry):
        for k in range(GROUP):
            action(peer_of(me, 1 + GROUP * j + k))
        return carry

    lax.fori_loop(0, (DEV - 2) // GROUP, several, 0)
    action(peer_of(me, DEV - 1))


def place(device):
    return (device // 64, lax.rem(device, 64))


def fused_kernel(counts, charges, splines, cells, *rest):
    sources, out = rest[:9], rest[9]
    lists, total_ref = rest[10:14], rest[14]
    held = rest[15:24]
    send1, arrive1, x_ref, send2, arrive2, turned, transposed, halfway, stage = rest[24:33]
    load_sem, send_sem, arrive1_sem, arrive2_sem, out_sem = rest[33:38]
    y_high, y_low, even_high, even_low, odd_high, odd_low, shuffle, unzip, green = held
    me = lax.axis_index("zg") * 64 + lax.axis_index("xy")
    barrier = pltpu.get_barrier_semaphore()

    loads = [
        pltpu.make_async_copy(source, target, load_sem.at[i])
        for i, (source, target) in enumerate(zip(sources, held))
    ]
    for load in loads:
        load.start()

    def greet(peer):
        pl.semaphore_signal(
            barrier, inc=1, device_id=place(peer), device_id_type=pl.DeviceIdType.MESH
        )

    each_peer(me, greet)
    prepare(counts, charges, splines, cells, *lists)

    def push(peer, source, target, sent, arrived):
        pltpu.make_async_remote_copy(
            src_ref=source,
            dst_ref=target,
            send_sem=sent,
            recv_sem=arrived,
            device_id=place(peer),
            device_id_type=pl.DeviceIdType.MESH,
        ).start()

    def await_all(most, sem):
        pltpu.make_async_copy(most, most, sem).wait()

    others = pl.ds(0, DEV - 1)

    def plane_body(plane, carry):
        density_of(plane, *lists, total_ref)

        @pl.when(plane == 0)
        def _():
            for load in loads[:6]:
                load.wait()
            pl.semaphore_wait(barrier, DEV - 1)

        folds = along_y(total_ref[...], y_high, y_low)
        send1[plane, :, 0] = along_x(folds[0], even_high, even_low)
        send1[plane, :, 1] = along_x(folds[1], odd_high, odd_low)
        each_peer(
            me,
            lambda peer: push(
                peer, send1.at[plane, peer], arrive1.at[me, plane], send_sem.at[0], arrive1_sem.at[plane]
            ),
        )
        arrive1[me, plane] = send1[plane, me]
        return carry

    lax.fori_loop(0, SLAB - 1, plane_body, 0)
    last = SLAB - 1
    density_of(last, *lists, total_ref)
    folds = along_y(total_ref[...], y_high, y_low)
    for q, tables in enumerate(((even_high, even_low), (odd_high, odd_low))):
        send1[last, :, q] = along_x(folds[q], *tables)
        each_peer(
            me,
            lambda peer: push(
                peer,
                send1.at[last, peer, q],
                arrive1.at[me, last, q],
                send_sem.at[0],
                arrive1_sem.at[last + q],
            ),
        )
        arrive1[me, last, q] = send1[last, me, q]

    transposed[0] = even_high[...].T
    transposed[1] = odd_high[...].T
    for load in loads[6:]:
        load.wait()
    for plane in range(last):
        await_all(arrive1.at[others, plane], arrive1_sem.at[plane])

    await_all(arrive1.at[others, last, 0], arrive1_sem.at[last])
    mix(0, green, shuffle, arrive1, send2, x_ref)
    each_peer(
        me,
        lambda peer: push(
            peer, send2.at[0, peer], arrive2.at[0, me], send_sem.at[1], arrive2_sem.at[SLAB]
        ),
    )
    arrive2[0, me] = send2[0, me]
    await_all(arrive1.at[others, last, 1], arrive1_sem.at[last + 1])
    mix(1, green, shuffle, arrive1, send2, x_ref)
    for plane in range(SLAB):
        each_peer(
            me,
            lambda peer: push(
                peer,
                send2.at[1, peer, plane],
                arrive2.at[1, me, plane],
                send_sem.at[1],
                arrive2_sem.at[plane],
            ),
        )
    arrive2[1, me] = send2[1, me]

    await_all(arrive2.at[0, others], arrive2_sem.at[SLAB])
    for plane in range(SLAB):
        halfway[plane] = back_along_x(0, plane, arrive2, unzip, transposed, turned)
    writes = [
        pltpu.make_async_copy(stage.at[plane], out.at[plane], out_sem.at[plane])
        for plane in range(SLAB)
    ]
    for plane in range(SLAB):
        await_all(arrive2.at[1, others, plane], arrive2_sem.at[plane])
        even = halfway[plane]
        odd = back_along_x(1, plane, arrive2, unzip, transposed, turned)
        middle = jnp.concatenate([even + odd, even - odd], axis=0).astype(BF16)
        stage[plane] = dot_nt(middle, y_high[...]) * (1.0 / 512.0)
        writes[plane].start()

    await_all(arrive1.at[others], send_sem.at[0])
    await_all(send2.at[:, others], send_sem.at[1])
    for write in writes:
        write.wait()


def tiles_side_by_side(tiles):
    return jnp.concatenate([tiles[:16].reshape(256, 128), tiles[16:].reshape(256, 128)], axis=1)


def mix(q, green, shuffle, arrived, out, x_ref):
    first = lax.broadcasted_iota(jnp.int32, (NZ, 128), 1) == 0

    def turn(g, carry):
        tiles = arrived[pl.ds(g * 32, 32), :, q].reshape(96, 16, 128)
        for j in range(3):
            block = tiles_side_by_side(tiles[32 * j : 32 * j + 32])
            rows = dot(shuffle[...], block).astype(BF16).reshape(16, 16, 256)
            for k in range(2):
                at = pl.ds(pl.multiple_of(g * 96 + j * 32 + k * 16, 16), 16)
                for h in range(2):
                    x_ref[q, :, at, 128 * h : 128 * h + 128] = rows[
                        8 * h : 8 * h + 8, :, 128 * k : 128 * k + 128
                    ]
        return carry

    lax.fori_loop(0, DEV // 32, turn, 0, unroll=4)

    def one_wave(r):
        rows = [r, r + 2, r + 4, r + 6]
        pr, pi, mr, mi = (x_ref[q, row] for row in rows)
        p0 = [pr[:, :128].astype(F32), pi[:, :128].astype(F32)]
        m0 = [mr[:, :128].astype(F32), mi[:, :128].astype(F32)]
        m1 = [mr[:, 128:].astype(F32), mi[:, 128:].astype(F32)]
        zero = [(p0[0] + m0[0]) * 0.5, (p0[1] + m0[1]) * 0.5]
        last = [(p0[1] - m0[1]) * 0.5, (m0[0] - p0[0]) * 0.5]
        pick = lambda a, b: jnp.concatenate(
            [jnp.where(first, x, y) for x, y in zip(a, b)], axis=1
        ).astype(BF16)
        block0 = pick(zero, p0)
        block1 = jnp.concatenate([pr[:, 128:], pi[:, 128:]], axis=1)
        block2 = pick(last, m1)
        block3 = pick(m1, m0)
        u = 2 * r + q
        y0, y1, y2, y3 = (
            dot(green[u, b], block) for b, block in enumerate((block0, block1, block2, block3))
        )
        re = lambda a: a[:, :128]
        im = lambda a: a[:, 128:]
        ar = jnp.where(first, (re(y0) - im(y2)) * 0.5, re(y0))
        ai = jnp.where(first, (im(y0) + re(y2)) * 0.5, im(y0))
        br = jnp.where(first, (re(y0) + im(y2)) * 0.5, re(y3))
        bi = jnp.where(first, (im(y0) - re(y2)) * 0.5, im(y3))
        cr = jnp.where(first, re(y3), re(y2))
        ci = jnp.where(first, im(y3), im(y2))
        x_ref[q, rows[0]] = jnp.concatenate([ar, re(y1)], axis=1).astype(BF16)
        x_ref[q, rows[1]] = jnp.concatenate([ai, im(y1)], axis=1).astype(BF16)
        x_ref[q, rows[2]] = jnp.concatenate([br, cr], axis=1).astype(BF16)
        x_ref[q, rows[3]] = jnp.concatenate([bi, ci], axis=1).astype(BF16)

    for r in range(2):
        one_wave(r)

    def turn_back(g, carry):
        tiles = []
        for j in range(3):
            pair = []
            for k in range(2):
                at = pl.ds(pl.multiple_of(g * 96 + j * 32 + k * 16, 16), 16)
                pair += [x_ref[q, :, at, :128], x_ref[q, :, at, 128:]]
            block = tiles_side_by_side(jnp.concatenate(pair, axis=0))
            rows = dot(shuffle[...], block).astype(BF16)
            tiles += [rows[:, :128].reshape(16, 16, 128), rows[:, 128:].reshape(16, 16, 128)]
        out[q, pl.ds(g * 32, 32)] = jnp.concatenate(tiles, axis=0).reshape(32, SLAB, 16, 128)
        return carry

    lax.fori_loop(0, DEV // 32, turn_back, 0, unroll=4)


def back_along_x(q, plane, arrived, unzip, transposed, turned):
    for g in range(DEV // 32):
        block = tiles_side_by_side(arrived[q, pl.ds(g * 32, 32), plane])
        rows = dot(unzip[...], block).astype(BF16)
        for k in range(2):
            for h in range(2):
                turned[q, g * 256 + k * 128 : g * 256 + k * 128 + 128, 128 * h : 128 * h + 128] = (
                    rows[128 * h : 128 * h + 128, 128 * k : 128 * k + 128]
                )
    out = dot(transposed[q], turned[q])
    return jnp.concatenate([out[:HALF], out[HALF:]], axis=1)


VMEM = pl.BlockSpec(memory_space=pltpu.VMEM)
ANY = pl.BlockSpec(memory_space=pl.ANY)


def shards(charges, cells, splines, counts, green):
    constants = [*make_tables(), make_shuffle(), make_unzip()]
    return pl.pallas_call(
        fused_kernel,
        out_shape=jax.ShapeDtypeStruct((SLAB, NX, NY), F32),
        in_specs=[pl.BlockSpec(memory_space=pltpu.SMEM)] + [VMEM] * 3 + [ANY] * 9,
        out_specs=ANY,
        scratch_shapes=[
            pltpu.VMEM((SPREAD, SLOTS), F32),
            pltpu.VMEM((SPREAD, SLOTS), F32),
            pltpu.VMEM((SPREAD, SLOTS), jnp.int32),
            pltpu.VMEM((SPREAD, SLOTS), jnp.int32),
            pltpu.VMEM((NX, NY), F32),
            *[pltpu.VMEM(table.shape, BF16) for table in constants],
            pltpu.VMEM(green.shape, BF16),
            pltpu.VMEM((SLAB, DEV, 2, 16, 128), BF16),
            pltpu.VMEM((DEV, SLAB, 2, 16, 128), BF16),
            pltpu.VMEM((2, 8, NZ, 256), BF16),
            pltpu.VMEM((2, DEV, SLAB, 16, 128), BF16),
            pltpu.VMEM((2, DEV, SLAB, 16, 128), BF16),
            pltpu.VMEM((2, DEV * 8, HALF), BF16),
            pltpu.VMEM((2, NX, DEV * 8), BF16),
            pltpu.VMEM((SLAB, HALF, NY), F32),
            pltpu.VMEM((SLAB, NX, NY), F32),
            pltpu.SemaphoreType.DMA((9,)),
            pltpu.SemaphoreType.DMA((2,)),
            pltpu.SemaphoreType.DMA((SLAB + 1,)),
            pltpu.SemaphoreType.DMA((SLAB + 1,)),
            pltpu.SemaphoreType.DMA((SLAB,)),
        ],
        compiler_params=pltpu.CompilerParams(
            collective_id=0, has_side_effects=True, vmem_limit_bytes=62 * 2**20
        ),
        name="fused",
    )(counts, charges.reshape(1, SLOTS), splines, cells, *constants, green)


def solution(mesh):
    in_specs = (
        P(("zg", "xy")),
        P(None, ("zg", "xy")),
        P(None, ("zg", "xy")),
        P(("zg", "xy")),
        P(("zg", "xy"), None, None, None),
    )
    out_specs = P(("zg", "xy"), None, None)
    return jax.shard_map(shards, mesh=mesh, in_specs=in_specs, out_specs=out_specs, check_vma=False)
```

time: 112 us -> 106 us (0.946)
  Pallas kernels: 111 us -> 101 us
  local copies, waits for them, and re-layouts: 0 us -> 3.86 us
    pallas_call x1, Pallas kernels: 106 us -> 101 us  [shards(): pl.pallas_call(fused_kernel, out_shape=jax.ShapeDtypeStruct((SLAB, NX, NY...]
    pallas_call x1 -> x0, Pallas kernels: 4.56 us -> none  [shards(): pl.pallas_call(back_along_y, grid=(SLAB,), out_shape=jax.ShapeDtypeStruct...]
    unnamed x0 -> x1, local copies, waits for them, and re-layouts: none -> 3.86 us
where the time goes in v4:
time: 106 us
  Pallas kernels  101 us (95%)
  local copies, waits for them, and re-layouts  3.86 us (4%)
    pallas_call x1, Pallas kernels, shards(): pl.pallas_call(fused_kernel, out_shape=jax.ShapeDtypeStruct((SLAB, NX, NY...  101 us
    unnamed x1, local copies, waits for them, and re-layouts  3.86 us

profile of v4, /device:TPU:1, one launch (start us, length us, event | category | flops | bytes accessed | tf_op | source)
XLA Modules:
  0.0 105.6 jit_solution(13279075858292495596)
XLA Ops:
  0.7 101.1 %fused.1 = f32[3,512,512]{2,1,0:T(8,128)} custom-call(s32[1]{0:T(128)S(6)} %copy.15.counts, f32[1,2048]{1,0:T(1,128)} %bitcast.1, f32[8,2048]{1,0:T(8,128)} %splines.1, s32[8,2048]{1,0:T(8,128)} %cells.1, bf16[512,512]{1,0:T(8,128)(2,1)} %constant.16.clone.rest_0_, bf16[512,512]{1,0:T(8,128)(2,1)} %constant.17.clone.rest_1_, ...), custom_call_target="tpu_custom_call" | custom-call | tf_op jit(solution)/shard_map/fused/pallas_call | solution.py:387
  101.7 3.9 %copy.16 = f32[3,512,512]{2,1,0:T(8,128)} copy(f32[3,512,512]{2,1,0:T(8,128)} %fused.1) | data formatting | bytes 6291456

commit v5 on v4

--- a/solution.py
+++ b/solution.py
@@ -19,8 +19,7 @@
 SPREAD = 8
 CHUNK = 1024
 CANDIDATES = 32
-STEP = 37
-GROUP = 9
+SHARES = SLOTS // CHUNK + 1
 F32 = jnp.float32
 BF16 = jnp.bfloat16
 
@@ -105,12 +104,14 @@
     col_ref[...] = lax.bitwise_and(cells[...], NY - 1)
 
 
-def density_of(plane, left_ref, right_ref, row_ref, col_ref, total_ref):
+def density_of(plane, left_ref, right_ref, row_ref, col_ref, total_ref, between=None):
     total_ref[...] = jnp.zeros_like(total_ref)
     index = lax.broadcasted_iota(jnp.int32, (NX, CHUNK), 0)
     index_row = index + plane * NX
 
     def body(c, carry):
+        if between is not None:
+            between(c)
         at = pl.ds(pl.multiple_of(c * CHUNK, CHUNK), CHUNK)
         a, b = [], []
         for k in range(SPREAD):
@@ -143,30 +144,35 @@
     return unzip.astype(BF16)
 
 
-def peer_of(me, i):
-    return lax.rem(me + STEP * i, DEV)
-
-
-def each_peer(me, action):
-    def several(j, carry):
-        for k in range(GROUP):
-            action(peer_of(me, 1 + GROUP * j + k))
-        return carry
-
-    lax.fori_loop(0, (DEV - 2) // GROUP, several, 0)
-    action(peer_of(me, DEV - 1))
-
-
-def place(device):
-    return (device // 64, lax.rem(device, 64))
+def far_first():
+    offsets = [o for o in np.ndindex(4, 4, 4, 2) if any(o)]
+    hops = lambda o: sum(min(d, 4 - d) for d in o[:3])
+    return sorted(offsets, key=lambda o: (-hops(o), o))
+
+
+def each_peer(action, share=0, shares=1):
+    low = lax.axis_index("zg")
+    index = lax.axis_index("xy")
+    along = 2 * (index // 32) + low
+    x = [lax.rem(along + d, 4) for d in range(4)]
+    x_low = [lax.rem(a, 2) for a in x]
+    x_high = [32 * (a // 2) for a in x]
+    y = [8 * lax.rem(lax.rem(index // 8, 4) + d, 4) for d in range(4)]
+    z = [2 * lax.rem(lax.rem(index // 2, 4) + d, 4) for d in range(4)]
+    core = [lax.rem(index + d, 2) for d in range(2)]
+    order = far_first()
+    each = -(-len(order) // shares)
+    for dx, dy, dz, dc in order[each * share : each * (share + 1)]:
+        inner = x_high[dx] + y[dy] + z[dz] + core[dc]
+        action(64 * x_low[dx] + inner, (x_low[dx], inner))
 
 
 def fused_kernel(counts, charges, splines, cells, *rest):
-    sources, out = rest[:9], rest[9]
-    lists, total_ref = rest[10:14], rest[14]
-    held = rest[15:24]
-    send1, arrive1, x_ref, send2, arrive2, turned, transposed, halfway, stage = rest[24:33]
-    load_sem, send_sem, arrive1_sem, arrive2_sem, out_sem = rest[33:38]
+    sources, out, middle_out = rest[:9], rest[9], rest[10]
+    lists, total_ref = rest[11:15], rest[15]
+    held = rest[16:25]
+    send1, arrive1, x_ref, send2, arrive2, turned, transposed, halfway, stage, middle = rest[25:35]
+    load_sem, send_sem, arrive1_sem, arrive2_sem, out_sem = rest[35:40]
     y_high, y_low, even_high, even_low, odd_high, odd_low, shuffle, unzip, green = held
     me = lax.axis_index("zg") * 64 + lax.axis_index("xy")
     barrier = pltpu.get_barrier_semaphore()
@@ -178,21 +184,21 @@
     for load in loads:
         load.start()
 
-    def greet(peer):
+    def greet(peer, place):
         pl.semaphore_signal(
-            barrier, inc=1, device_id=place(peer), device_id_type=pl.DeviceIdType.MESH
-        )
-
-    each_peer(me, greet)
+            barrier, inc=1, device_id=place, device_id_type=pl.DeviceIdType.MESH
+        )
+
+    each_peer(greet)
     prepare(counts, charges, splines, cells, *lists)
 
-    def push(peer, source, target, sent, arrived):
+    def push(place, source, target, sent, arrived):
         pltpu.make_async_remote_copy(
             src_ref=source,
             dst_ref=target,
             send_sem=sent,
             recv_sem=arrived,
-            device_id=place(peer),
+            device_id=place,
             device_id_type=pl.DeviceIdType.MESH,
         ).start()
 
@@ -201,37 +207,45 @@
 
     others = pl.ds(0, DEV - 1)
 
-    def plane_body(plane, carry):
-        density_of(plane, *lists, total_ref)
-
-        @pl.when(plane == 0)
-        def _():
+    def send_plane(plane, share, shares):
+        each_peer(
+            lambda peer, place: push(
+                place, send1.at[plane, peer], arrive1.at[me, plane], send_sem.at[0], arrive1_sem.at[plane]
+            ),
+            share,
+            shares,
+        )
+
+    def send_between(plane):
+        def between(c):
+            for share in range(SLOTS // CHUNK):
+
+                @pl.when(c == share)
+                def _():
+                    send_plane(plane, share, SHARES)
+
+        return between
+
+    last = SLAB - 1
+    for plane in range(SLAB):
+        density_of(plane, *lists, total_ref, send_between(plane - 1) if plane else None)
+        if plane > 0:
+            send_plane(plane - 1, SHARES - 1, SHARES)
+        if plane == 0:
             for load in loads[:6]:
                 load.wait()
             pl.semaphore_wait(barrier, DEV - 1)
-
-        folds = along_y(total_ref[...], y_high, y_low)
-        send1[plane, :, 0] = along_x(folds[0], even_high, even_low)
-        send1[plane, :, 1] = along_x(folds[1], odd_high, odd_low)
-        each_peer(
-            me,
-            lambda peer: push(
-                peer, send1.at[plane, peer], arrive1.at[me, plane], send_sem.at[0], arrive1_sem.at[plane]
-            ),
-        )
-        arrive1[me, plane] = send1[plane, me]
-        return carry
-
-    lax.fori_loop(0, SLAB - 1, plane_body, 0)
-    last = SLAB - 1
-    density_of(last, *lists, total_ref)
+        if plane < last:
+            folds = along_y(total_ref[...], y_high, y_low)
+            send1[plane, :, 0] = along_x(folds[0], even_high, even_low)
+            send1[plane, :, 1] = along_x(folds[1], odd_high, odd_low)
+            arrive1[me, plane] = send1[plane, me]
     folds = along_y(total_ref[...], y_high, y_low)
     for q, tables in enumerate(((even_high, even_low), (odd_high, odd_low))):
         send1[last, :, q] = along_x(folds[q], *tables)
         each_peer(
-            me,
-            lambda peer: push(
-                peer,
+            lambda peer, place: push(
+                place,
                 send1.at[last, peer, q],
                 arrive1.at[me, last, q],
                 send_sem.at[0],
@@ -250,9 +264,8 @@
     await_all(arrive1.at[others, last, 0], arrive1_sem.at[last])
     mix(0, green, shuffle, arrive1, send2, x_ref)
     each_peer(
-        me,
-        lambda peer: push(
-            peer, send2.at[0, peer], arrive2.at[0, me], send_sem.at[1], arrive2_sem.at[SLAB]
+        lambda peer, place: push(
+            place, send2.at[0, peer], arrive2.at[0, me], send_sem.at[1], arrive2_sem.at[SLAB]
         ),
     )
     arrive2[0, me] = send2[0, me]
@@ -260,9 +273,8 @@
     mix(1, green, shuffle, arrive1, send2, x_ref)
     for plane in range(SLAB):
         each_peer(
-            me,
-            lambda peer: push(
-                peer,
+            lambda peer, place: push(
+                place,
                 send2.at[1, peer, plane],
                 arrive2.at[1, me, plane],
                 send_sem.at[1],
@@ -276,14 +288,17 @@
         halfway[plane] = back_along_x(0, plane, arrive2, unzip, transposed, turned)
     writes = [
         pltpu.make_async_copy(stage.at[plane], out.at[plane], out_sem.at[plane])
-        for plane in range(SLAB)
-    ]
+        for plane in range(last)
+    ] + [pltpu.make_async_copy(middle, middle_out, out_sem.at[last])]
     for plane in range(SLAB):
         await_all(arrive2.at[1, others, plane], arrive2_sem.at[plane])
         even = halfway[plane]
         odd = back_along_x(1, plane, arrive2, unzip, transposed, turned)
-        middle = jnp.concatenate([even + odd, even - odd], axis=0).astype(BF16)
-        stage[plane] = dot_nt(middle, y_high[...]) * (1.0 / 512.0)
+        value = jnp.concatenate([even + odd, even - odd], axis=0).astype(BF16)
+        if plane < last:
+            stage[plane] = dot_nt(value, y_high[...]) * (1.0 / 512.0)
+        else:
+            middle[...] = value
         writes[plane].start()
 
     await_all(arrive1.at[others], send_sem.at[0])
@@ -378,17 +393,45 @@
     return jnp.concatenate([out[:HALF], out[HALF:]], axis=1)
 
 
+def finish_kernel(part, middle, y_high, out, middle_ref, y_ref, stage, load_sem, write_sem):
+    last = SLAB - 1
+    loads = [
+        pltpu.make_async_copy(source, target, load_sem.at[i])
+        for i, (source, target) in enumerate(
+            ((part.at[0], stage.at[0]), (part.at[1], stage.at[1]), (middle, middle_ref), (y_high, y_ref))
+        )
+    ]
+    writes = [
+        pltpu.make_async_copy(stage.at[plane], out.at[plane], write_sem.at[plane])
+        for plane in range(SLAB)
+    ]
+    for load in loads:
+        load.start()
+    for plane in range(last):
+        loads[plane].wait()
+        writes[plane].start()
+    loads[2].wait()
+    loads[3].wait()
+    stage[last] = dot_nt(middle_ref[...], y_ref[...]) * (1.0 / 512.0)
+    writes[last].start()
+    for write in writes:
+        write.wait()
+
+
 VMEM = pl.BlockSpec(memory_space=pltpu.VMEM)
 ANY = pl.BlockSpec(memory_space=pl.ANY)
 
 
 def shards(charges, cells, splines, counts, green):
     constants = [*make_tables(), make_shuffle(), make_unzip()]
-    return pl.pallas_call(
+    part, middle = pl.pallas_call(
         fused_kernel,
-        out_shape=jax.ShapeDtypeStruct((SLAB, NX, NY), F32),
+        out_shape=(
+            jax.ShapeDtypeStruct((SLAB - 1, NX, NY), F32),
+            jax.ShapeDtypeStruct((NX, NY), BF16),
+        ),
         in_specs=[pl.BlockSpec(memory_space=pltpu.SMEM)] + [VMEM] * 3 + [ANY] * 9,
-        out_specs=ANY,
+        out_specs=(ANY, ANY),
         scratch_shapes=[
             pltpu.VMEM((SPREAD, SLOTS), F32),
             pltpu.VMEM((SPREAD, SLOTS), F32),
@@ -405,7 +448,8 @@
             pltpu.VMEM((2, DEV * 8, HALF), BF16),
             pltpu.VMEM((2, NX, DEV * 8), BF16),
             pltpu.VMEM((SLAB, HALF, NY), F32),
-            pltpu.VMEM((SLAB, NX, NY), F32),
+            pltpu.VMEM((SLAB - 1, NX, NY), F32),
+            pltpu.VMEM((NX, NY), BF16),
             pltpu.SemaphoreType.DMA((9,)),
             pltpu.SemaphoreType.DMA((2,)),
             pltpu.SemaphoreType.DMA((SLAB + 1,)),
@@ -417,6 +461,20 @@
         ),
         name="fused",
     )(counts, charges.reshape(1, SLOTS), splines, cells, *constants, green)
+    return pl.pallas_call(
+        finish_kernel,
+        out_shape=jax.ShapeDtypeStruct((SLAB, NX, NY), F32),
+        in_specs=[ANY] * 3,
+        out_specs=ANY,
+        scratch_shapes=[
+            pltpu.VMEM((NX, NY), BF16),
+            pltpu.VMEM((NY, NY), BF16),
+            pltpu.VMEM((SLAB, NX, NY), F32),
+            pltpu.SemaphoreType.DMA((4,)),
+            pltpu.SemaphoreType.DMA((SLAB,)),
+        ],
+        name="finish",
+    )(part, middle, constants[0])
 
 
 def solution(mesh):

time: 106 us -> 104 us (0.981)
  local copies, waits for them, and re-layouts: 3.86 us -> 0 us
  Pallas kernels: 101 us -> 103 us
    unnamed x1 -> x0, local copies, waits for them, and re-layouts: 3.86 us -> none
    pallas_call x1 -> x2, Pallas kernels: 101 us -> 103 us  [the longest x1 99.7 us: shards(): pl.pallas_call(fused_kernel, out_shape=(jax.ShapeDtypeStruct((SLAB - 1, N...]
where the time goes in v5:
time: 104 us
  Pallas kernels  103 us (99%)
    pallas_call x1, Pallas kernels, shards(): pl.pallas_call(fused_kernel, out_shape=(jax.ShapeDtypeStruct((SLAB - 1, N...  99.7 us
    pallas_call x1, Pallas kernels, shards(): pl.pallas_call(finish_kernel, out_shape=jax.ShapeDtypeStruct((SLAB, NX, N...  3.33 us

profile of v5, /device:TPU:1, one launch (start us, length us, event | category | flops | bytes accessed | tf_op | source)
XLA Modules:
  0.0 103.9 jit_solution(12336722749953317407)
XLA Ops:
  0.7 99.7 %fused.1 = (f32[2,512,512]{2,1,0:T(8,128)}, bf16[512,512]{1,0:T(8,128)(2,1)}) custom-call(s32[1]{0:T(128)S(6)} %copy.14.counts, f32[1,2048]{1,0:T(1,128)} %bitcast.1, f32[8,2048]{1,0:T(8,128)} %splines.1, s32[8,2048]{1,0:T(8,128)} %cells.1, bf16[512,512]{1,0:T(8,128)(2,1)} %constant.16.clone.rest_0_.y_high, bf16[512,512]{1,0:T(8,128)(2,1)} %constant.17.clone.rest_1_, ...), custom_call_target="tpu_custom_call" | custom-call | tf_op jit(solution)/shard_map/fused/pallas_call | solution.py:427
  100.4 3.3 %finish.1 = f32[3,512,512]{2,1,0:T(8,128)} custom-call(f32[2,512,512]{2,1,0:T(8,128)} %get-tuple-element.7.part, bf16[512,512]{1,0:T(8,128)(2,1)} %get-tuple-element.8.middle, bf16[512,512]{1,0:T(8,128)(2,1)} %constant.16.clone.rest_0_.y_high), custom_call_target="tpu_custom_call" | custom-call | tf_op jit(solution)/shard_map/finish/pallas_call | solution.py:464
